TPU v7x, 32 devices: a whole 2x2x4 slice. The times are simulated.
32 devices in a mesh: parts: 2 (over y), replica: 4 (over x, core), tensor: 4 (over z).
Axes of the slice: x: 2, y: 2, z: 4, core: 2. Of those that a mesh axis runs over, the one named last changes fastest.
Arguments:
- prompt_owner: int32 [8], P('parts'), parts along dimension 0, may hold values from 0 to 3, each once
- fork_map: int32 [1024], P(('parts', 'replica')), parts along dimension 0, may hold values from 0 to 3
- page_table: int32 [24], P('parts'), parts along dimension 0, may hold values from 0 to 11, each once
- prompt_length: int32 [8], P('parts'), parts along dimension 0, may hold values from 1 to 384
- span_states: bfloat16 [1024, 8192], P(('parts', 'replica'), 'tensor'), parts along dimension 0, may hold values from -6 to 6
- decode_states: bfloat16 [1024, 4, 8192], P(('parts', 'replica'), None, 'tensor'), parts along dimension 0, may hold values from -6 to 6
- decode_queries: bfloat16 [1024, 4, 4096], P(('parts', 'replica'), None, 'tensor'), parts along dimension 0, may hold values from -64 to 64
- key_weight: bfloat16 [8192, 512], P('tensor'), may hold values from -0.0625 to 0.0625
- value_weight: bfloat16 [8192, 512], P('tensor'), may hold values from -0.0625 to 0.0625
- out_weight: bfloat16 [4096, 8192], P(None, 'tensor'), may hold values from -0.09375 to 0.09375
- page_pool: bfloat16 [4, 24, 128, 256], P('tensor', 'parts'), parts along dimension 1, may hold values from -6 to 60, as said below
Outputs:
- decoded: bfloat16 [1024, 4, 8192], P(('parts', 'replica'), None, 'tensor'), parts along dimension 0
There are 2 independent parts, one for each index of `parts`. A program takes and returns all parts, laid end to end along the dimension named above; an argument that names none is the same for every part. Nothing has to cross between parts.
Inputs may be any that keep to these rules, and one draw needn't show every extreme that they name: Replica r prefills prompt prompt_owner[r]; every prompt has exactly one such replica. The cache pages of prompt p are page_table[p * 3 + c] for c below 3; every pool page belongs to exactly one prompt. page_pool[t] holds the cache of key-value head t; devices that read the same head hold equal copies.
All inputs are finite; a program needn't handle non-finite values.
Results may differ from a plain program's by a relative error of at most 0.009.
Values may be sent and summed in bfloat16 or wider, within the bound.
A program may use at most 64 MiB of HBM per device.

v0:
```python
import functools
import math

import jax
import jax.numpy as jnp
from jax import lax
from jax.experimental import pallas as pl
from jax.experimental.pallas import tpu as pltpu
from jax.sharding import PartitionSpec as P

HD = 128


rope_base = 1000000.0


def rotary(vectors, places):
    half = vectors.shape[-1] // 2
    freq = rope_base ** (-(2.0 / vectors.shape[-1]) * jnp.arange(half, dtype=jnp.float32))
    angle = places.astype(jnp.float32)[..., None, None] * freq
    cosine = jnp.cos(angle)
    sine = jnp.sin(angle)
    first = vectors[..., :half]
    second = vectors[..., half:]
    return jnp.concatenate([first * cosine - second * sine, second * cosine + first * sine], -1)


def rotate_round(summed, places, kv_heads):
    number = summed.shape[0]
    turned = rotary(summed[:, : kv_heads * HD].reshape(number, kv_heads, HD), places)
    turned = turned.astype(jnp.bfloat16).reshape(number, kv_heads * HD)
    return jnp.concatenate([turned, summed[:, kv_heads * HD :].astype(jnp.bfloat16)], 1)


def own_pair(packed, head_group, kv_heads):
    key_part = lax.dynamic_slice_in_dim(packed, head_group * HD, HD, 1)
    value_part = lax.dynamic_slice_in_dim(packed, (kv_heads + head_group) * HD, HD, 1)
    return jnp.concatenate([key_part, value_part], 1)


def general(
    prompt_owner,
    fork_map,
    page_table,
    prompt_length,
    span_states,
    decode_states,
    decode_queries,
    key_weight,
    value_weight,
    out_weight,
    page_pool,
):
    replica = lax.axis_index("replica")
    device_rank = lax.axis_index("tensor")
    n_replica = lax.axis_size("replica")
    n_tensor = lax.axis_size("tensor")
    span = span_states.shape[0]
    rows, steps, width = decode_states.shape
    heads_dev = decode_queries.shape[2] // HD
    kv_heads = key_weight.shape[1] // HD
    sharing = n_tensor // kv_heads
    prompts = jnp.arange(n_replica, dtype=jnp.int32)
    own_prompt = jnp.sum(jnp.where(prompts == replica, prompt_owner, 0))
    own_length = jnp.sum(jnp.where(prompts == own_prompt, prompt_length, 0))
    row_hits = fork_map[:, None] == prompts[None, :]
    row_length = jnp.sum(jnp.where(row_hits, prompt_length[None, :], 0), 1)
    positions = jnp.concatenate(
        [
            own_length + jnp.arange(span, dtype=jnp.int32),
            (row_length[:, None] + span + jnp.arange(steps, dtype=jnp.int32)[None, :]).reshape(-1),
        ]
    )
    tokens = jnp.concatenate([span_states, decode_states.reshape(rows * steps, width)], 0)
    projected = jnp.dot(
        tokens, jnp.concatenate([key_weight, value_weight], 1), preferred_element_type=jnp.float32
    )
    share = lax.psum_scatter(projected, "tensor", scatter_dimension=0, tiled=True)
    number = share.shape[0]
    start = device_rank * number
    places = lax.dynamic_slice_in_dim(positions, start, number)
    turned = rotate_round(share, places, kv_heads)
    groups = jnp.stack(
        [own_pair(turned, group_index, kv_heads) for group_index in range(kv_heads)], 0
    )
    outgoing = jnp.repeat(groups, sharing, axis=0)
    paired = lax.all_to_all(outgoing, "tensor", split_axis=0, concat_axis=1, tiled=True).reshape(
        -1, 2 * HD
    )
    arrived = lax.all_gather(paired[:span], "replica", axis=0, tiled=True)
    tail_pair = paired[span:].reshape(rows, steps, 2 * HD)
    pool_pages = page_table.shape[0]
    cpages = pool_pages // n_replica
    page_size = page_pool.shape[2]
    entries = jnp.arange(pool_pages, dtype=jnp.int32)
    page_hits = page_table[None, :] == entries[:, None]
    page_prompt = jnp.sum(jnp.where(page_hits, entries[None, :] // cpages, 0), 1)
    page_slot = jnp.sum(jnp.where(page_hits, entries[None, :] % cpages, 0), 1)
    page_length = jnp.sum(
        jnp.where(page_prompt[:, None] == prompts[None, :], prompt_length[None, :], 0), 1
    )
    visible = (
        page_slot[:, None] * page_size + jnp.arange(page_size, dtype=jnp.int32)[None, :]
        < page_length[:, None]
    )
    pool_prompt = jnp.where(visible, page_prompt[:, None], -1).reshape(-1)
    key_prompt = jnp.concatenate([pool_prompt, jnp.repeat(prompt_owner, span)])
    key_table = jnp.concatenate([page_pool.reshape(-1, 2 * HD), arrived], 0)
    cached_keys = key_table[:, :HD]
    cached_values = key_table[:, HD:]
    scale = 1.0 / math.sqrt(HD)
    causal = jnp.arange(steps)[None, :] <= jnp.arange(steps)[:, None]
    per_block = max(1, min(rows, 512 // (steps * heads_dev)))
    blocks = rows // per_block
    queries = decode_queries.reshape(blocks, per_block, steps, heads_dev, HD)

    def attend(items):
        query, prompt, own_tail = items
        flat = query.reshape(-1, HD)
        scores = (
            lax.dot_general(
                flat, cached_keys, (((1,), (1,)), ((), ())), preferred_element_type=jnp.float32
            )
            * scale
        )
        scores = scores.reshape(per_block, steps, heads_dev, -1)
        allowed = (key_prompt[None, :] == prompt[:, None])[:, None, None, :]
        scores = jnp.where(allowed, scores, -jnp.inf)
        tail_scores = (
            jnp.einsum(
                "rshd,rtd->rsht", query, own_tail[..., :HD], preferred_element_type=jnp.float32
            )
            * scale
        )
        tail_scores = jnp.where(causal[None, :, None, :], tail_scores, -jnp.inf)
        highest = jnp.maximum(jnp.max(scores, -1), jnp.max(tail_scores, -1))
        weight = jnp.exp(scores - highest[..., None])
        tail_weight = jnp.exp(tail_scores - highest[..., None])
        total = jnp.sum(weight, -1) + jnp.sum(tail_weight, -1)
        rounded = weight.astype(jnp.bfloat16).reshape(-1, weight.shape[-1])
        mixed = jnp.dot(rounded, cached_values, preferred_element_type=jnp.float32).reshape(
            per_block, steps, heads_dev, HD
        )
        mixed = mixed + jnp.einsum(
            "rsht,rtd->rshd",
            tail_weight.astype(jnp.bfloat16),
            own_tail[..., HD:],
            preferred_element_type=jnp.float32,
        )
        return (mixed / total[..., None]).astype(jnp.bfloat16)

    attended = lax.map(
        attend,
        (
            queries,
            fork_map.reshape(blocks, per_block),
            tail_pair.reshape(blocks, per_block, steps, 2 * HD),
        ),
    )
    head_rows = attended.reshape(rows * steps, heads_dev * HD)
    decoded = jnp.dot(
        lax.all_gather(head_rows, "tensor", axis=1, tiled=True),
        out_weight,
        preferred_element_type=jnp.float32,
    )
    return decoded.astype(jnp.bfloat16).reshape(rows, steps, width)


MESH_ID = pl.DeviceIdType.MESH
TILE = 128
FAR = -(2.0**100)


def nt(left, right):
    return lax.dot_general(
        left, right, (((1,), (1,)), ((), ())), preferred_element_type=jnp.float32
    )


def fused(
    n, n_rep, steps, tok, wk, wv, cosine, sine, query, hot, pool, far, w_hbm, out,
    w_all, part, landed, own, span_all, keys, values, tail_key, tail_value, gathered, acc,
    w_sem, rs_send, rs_recv, sp_send, sp_recv, ag_send, ag_recv,
):
    z = lax.axis_index("tensor")
    rep = lax.axis_index("replica")
    span = span_all.shape[1]
    rows = query.shape[0]
    width = query.shape[1]
    heads = width // HD
    cached = pool.shape[0]
    blocks = tok.shape[0] // TILE
    span_blocks = span // TILE
    chunks = rows // TILE

    w_copy = pltpu.make_async_copy(w_hbm, w_all, w_sem)
    w_copy.start()
    barrier = pltpu.get_barrier_semaphore()
    for k in range(1, n):
        pl.semaphore_signal(
            barrier, inc=1, device_id={"tensor": lax.rem(z + k, n)}, device_id_type=MESH_ID
        )
    for k in range(1, n_rep):
        pl.semaphore_signal(
            barrier, inc=1, device_id={"replica": lax.rem(rep + k, n_rep)}, device_id_type=MESH_ID
        )
    pl.semaphore_wait(barrier, n + n_rep - 2)

    def at(block):
        return pl.ds(pl.multiple_of(block * TILE, TILE), TILE)

    def rs_copy(k, block):
        return pltpu.make_async_remote_copy(
            src_ref=part.at[k - 1, at(block)],
            dst_ref=landed.at[k - 1, at(block)],
            send_sem=rs_send.at[k - 1, block],
            recv_sem=rs_recv.at[k - 1, block],
            device_id={"tensor": lax.rem(z + k, n)},
            device_id_type=MESH_ID,
        )

    def project(block, owner):
        column = pl.ds(pl.multiple_of(owner * HD, HD), HD)
        weight = jnp.concatenate([wk[:, column], wv[:, column]], 1)
        return jnp.dot(tok[at(block), :], weight, preferred_element_type=jnp.float32)

    @pl.loop(0, blocks)
    def _(block):
        for k in range(1, n):
            part[k - 1, at(block), :] = project(block, lax.rem(z + k, n)).astype(jnp.bfloat16)
            rs_copy(k, block).start()

    @pl.loop(0, blocks)
    def _(block):
        own[at(block), :] = project(block, z)

    keys[:cached, :HD] = pool[:, :HD]
    values[:cached, :HD] = pool[:, HD:]
    keys[:, HD:] = far[...]
    values[:, HD:] = jnp.ones((values.shape[0], HD), jnp.bfloat16)
    tail_value[:, HD:] = jnp.ones((TILE, HD), jnp.bfloat16)

    def reduced(block):
        total = own[at(block), :]
        for k in range(1, n):
            rs_copy(k, block).wait_recv()
            total = total + landed[k - 1, at(block), :].astype(jnp.float32)
        key = total[:, :HD]
        key = key * cosine[at(block), :] + pltpu.roll(key, HD // 2, 1) * sine[at(block), :]
        return key.astype(jnp.bfloat16), total[:, HD:].astype(jnp.bfloat16)

    @pl.loop(0, span_blocks)
    def _(block):
        key, value = reduced(block)
        span_all[rep, at(block), :HD] = key
        span_all[rep, at(block), HD:] = value

    def sp_copy(k, whose):
        return pltpu.make_async_remote_copy(
            src_ref=span_all.at[whose],
            dst_ref=span_all.at[whose],
            send_sem=sp_send.at[k - 1],
            recv_sem=sp_recv.at[k - 1],
            device_id={"replica": lax.rem(rep + k, n_rep)},
            device_id_type=MESH_ID,
        )

    for k in range(1, n_rep):
        sp_copy(k, rep).start()
    for k in range(1, n_rep):
        sp_copy(k, lax.rem(rep - k + n_rep, n_rep)).wait_recv()
    for p in range(n_rep):
        keys[cached + p * span : cached + (p + 1) * span, :HD] = span_all[p, :, :HD]
        values[cached + p * span : cached + (p + 1) * span, :HD] = span_all[p, :, HD:]

    def ag_copy(side, distance, chunk, origin):
        target = z + 1 if side == 0 else z - 1
        return pltpu.make_async_remote_copy(
            src_ref=gathered.at[origin, at(chunk)],
            dst_ref=gathered.at[origin, at(chunk)],
            send_sem=ag_send.at[side, distance - 1, chunk],
            recv_sem=ag_recv.at[side, distance - 1, chunk],
            device_id={"tensor": target},
            device_id_type=MESH_ID,
        )

    line = lax.broadcasted_iota(jnp.int32, (TILE, TILE), 0)
    lane = lax.broadcasted_iota(jnp.int32, (TILE, TILE), 1)
    causal = (line // steps == lane // steps) & (lane <= line)
    factor = math.log2(math.e) / math.sqrt(HD)

    @pl.loop(0, chunks)
    def _(chunk):
        key, value = reduced(chunk + span_blocks)
        tail_key[...] = key
        tail_value[:, :HD] = value

        @pl.loop(0, heads)
        def _(head):
            column = pl.ds(pl.multiple_of(head * HD, HD), HD)
            asked = query[at(chunk), column]
            scores = nt(jnp.concatenate([asked, hot[at(chunk), :]], 1), keys[...])
            tail = jnp.where(causal, nt(asked, tail_key[...]), FAR)
            highest = jnp.maximum(
                jnp.max(scores, 1, keepdims=True), jnp.max(tail, 1, keepdims=True)
            )
            weight = jnp.exp2((scores - highest) * factor).astype(jnp.bfloat16)
            tail_weight = jnp.exp2((tail - highest) * factor).astype(jnp.bfloat16)
            mixed = jnp.dot(weight, values[...], preferred_element_type=jnp.float32) + jnp.dot(
                tail_weight, tail_value[...], preferred_element_type=jnp.float32
            )
            gathered[z, at(chunk), column] = (mixed[:, :HD] / mixed[:, HD:]).astype(jnp.bfloat16)

        @pl.when(z + 1 < n)
        def _():
            ag_copy(0, 1, chunk, z).start()

        @pl.when(z > 0)
        def _():
            ag_copy(1, 1, chunk, z).start()

    w_copy.wait()
    tall = min(2 * TILE, rows)
    per = tall // TILE
    wide = min(512, out.shape[1])

    def add(origin, half, first):
        span_rows = pl.ds(pl.multiple_of(half * tall, tall), tall)
        deep = pl.ds(pl.multiple_of(origin * width, width), width)

        @pl.loop(0, out.shape[1] // wide)
        def _(column):
            cols = pl.ds(pl.multiple_of(column * wide, wide), wide)
            term = jnp.dot(
                gathered[origin, span_rows, :], w_all[deep, cols], preferred_element_type=jnp.float32
            )
            if first:
                acc[span_rows, cols] = term
            else:
                acc[span_rows, cols] += term

    @pl.loop(0, rows // tall)
    def _(half):
        add(z, half, True)

    for distance in range(1, n):

        @pl.loop(0, rows // tall)
        def _(half):
            for side, origin, inside, onward in (
                (0, z - distance, z >= distance, z + 1 < n),
                (1, z + distance, z + distance < n, z > 0),
            ):
                for piece in range(per):
                    chunk = half * per + piece

                    @pl.when(inside)
                    def _():
                        ag_copy(side, distance, chunk, origin).wait_recv()

                    if distance < n - 1:

                        @pl.when(inside & onward)
                        def _():
                            ag_copy(side, distance + 1, chunk, origin).start()

            for side, origin, inside in (
                (0, z - distance, z >= distance),
                (1, z + distance, z + distance < n),
            ):

                @pl.when(inside)
                def _():
                    add(origin, half, False)

    @pl.loop(0, chunks)
    def _(chunk):
        out[at(chunk), :] = acc[at(chunk), :].astype(jnp.bfloat16)

    for k in range(1, n):

        @pl.loop(0, blocks)
        def _(block):
            rs_copy(k, block).wait_send()

    for k in range(1, n_rep):
        sp_copy(k, rep).wait_send()
    for distance in range(1, n):

        @pl.loop(0, chunks)
        def _(chunk):
            @pl.when((z >= distance - 1) & (z + 1 < n))
            def _():
                ag_copy(0, distance, chunk, z - distance + 1).wait_send()

            @pl.when((z + distance - 1 < n) & (z > 0))
            def _():
                ag_copy(1, distance, chunk, z + distance - 1).wait_send()


def on_device(
    prompt_owner,
    fork_map,
    page_table,
    prompt_length,
    span_states,
    decode_states,
    decode_queries,
    key_weight,
    value_weight,
    out_weight,
    page_pool,
):
    replica = lax.axis_index("replica")
    n_replica = lax.axis_size("replica")
    n_tensor = lax.axis_size("tensor")
    span = span_states.shape[0]
    rows, steps, width = decode_states.shape
    heads_dev = decode_queries.shape[2] // HD
    kv_heads = key_weight.shape[1] // HD
    number = rows * steps
    if (
        kv_heads != n_tensor
        or span % TILE
        or number % TILE
        or number % min(2 * TILE, number)
        or TILE % steps
        or n_replica > HD
    ):
        return general(
            prompt_owner, fork_map, page_table, prompt_length, span_states, decode_states,
            decode_queries, key_weight, value_weight, out_weight, page_pool,
        )
    prompts = jnp.arange(n_replica, dtype=jnp.int32)
    own_prompt = jnp.sum(jnp.where(prompts == replica, prompt_owner, 0))
    own_length = jnp.sum(jnp.where(prompts == own_prompt, prompt_length, 0))
    row_hits = fork_map[:, None] == prompts[None, :]
    row_length = jnp.sum(jnp.where(row_hits, prompt_length[None, :], 0), 1)
    positions = jnp.concatenate(
        [
            own_length + jnp.arange(span, dtype=jnp.int32),
            (row_length[:, None] + span + jnp.arange(steps, dtype=jnp.int32)[None, :]).reshape(-1),
        ]
    )
    half = HD // 2
    freq = rope_base ** (-(2.0 / HD) * jnp.arange(half, dtype=jnp.float32))
    angle = positions.astype(jnp.float32)[:, None] * freq
    cosine = jnp.cos(angle)
    sine = jnp.sin(angle)
    cosine = jnp.concatenate([cosine, cosine], 1)
    sine = jnp.concatenate([-sine, sine], 1)
    tokens = jnp.concatenate([span_states, decode_states.reshape(number, width)], 0)
    pool_pages = page_table.shape[0]
    cpages = pool_pages // n_replica
    page_size = page_pool.shape[2]
    entries = jnp.arange(pool_pages, dtype=jnp.int32)
    page_hits = page_table[None, :] == entries[:, None]
    page_prompt = jnp.sum(jnp.where(page_hits, entries[None, :] // cpages, 0), 1)
    page_slot = jnp.sum(jnp.where(page_hits, entries[None, :] % cpages, 0), 1)
    page_length = jnp.sum(
        jnp.where(page_prompt[:, None] == prompts[None, :], prompt_length[None, :], 0), 1
    )
    visible = (
        page_slot[:, None] * page_size + jnp.arange(page_size, dtype=jnp.int32)[None, :]
        < page_length[:, None]
    )
    pool_prompt = jnp.where(visible, page_prompt[:, None], -1).reshape(-1)
    key_prompt = jnp.concatenate([pool_prompt, jnp.repeat(prompt_owner, span)])
    lanes = jnp.arange(HD, dtype=jnp.int32)
    far = jnp.where(
        (lanes[None, :] < n_replica) & (key_prompt[:, None] != lanes[None, :]), FAR, 0.0
    ).astype(jnp.bfloat16)
    hot = jnp.broadcast_to(
        (fork_map[:, None] == lanes[None, :])[:, None, :], (rows, steps, HD)
    ).reshape(number, HD).astype(jnp.bfloat16)
    pool = page_pool.reshape(-1, 2 * HD)
    query = decode_queries.reshape(number, heads_dev * HD)
    features = out_weight.shape[1]
    table = pool.shape[0] + n_replica * span
    total = span + number
    vmem = pl.BlockSpec(memory_space=pltpu.VMEM)
    bf16, f32 = jnp.bfloat16, jnp.float32
    decoded = pl.pallas_call(
        functools.partial(fused, n_tensor, n_replica, steps),
        name="fused",
        out_shape=jax.ShapeDtypeStruct((number, features), bf16),
        in_specs=[vmem] * 9 + [pl.BlockSpec(memory_space=pl.ANY)],
        out_specs=vmem,
        scratch_shapes=[
            pltpu.VMEM(out_weight.shape, bf16),
            pltpu.VMEM((n_tensor - 1, total, 2 * HD), bf16),
            pltpu.VMEM((n_tensor - 1, total, 2 * HD), bf16),
            pltpu.VMEM((total, 2 * HD), f32),
            pltpu.VMEM((n_replica, span, 2 * HD), bf16),
            pltpu.VMEM((table, 2 * HD), bf16),
            pltpu.VMEM((table, 2 * HD), bf16),
            pltpu.VMEM((TILE, HD), bf16),
            pltpu.VMEM((TILE, 2 * HD), bf16),
            pltpu.VMEM((n_tensor, number, heads_dev * HD), bf16),
            pltpu.VMEM((number, features), f32),
            pltpu.SemaphoreType.DMA,
            pltpu.SemaphoreType.DMA((n_tensor - 1, total // TILE)),
            pltpu.SemaphoreType.DMA((n_tensor - 1, total // TILE)),
            pltpu.SemaphoreType.DMA((n_replica - 1,)),
            pltpu.SemaphoreType.DMA((n_replica - 1,)),
            pltpu.SemaphoreType.DMA((2, n_tensor - 1, number // TILE)),
            pltpu.SemaphoreType.DMA((2, n_tensor - 1, number // TILE)),
        ],
        compiler_params=pltpu.CompilerParams(
            collective_id=0, has_side_effects=True, vmem_limit_bytes=60 * 1024 * 1024
        ),
    )(tokens, key_weight, value_weight, cosine, sine, query, hot, pool, far, out_weight)
    return decoded.reshape(rows, steps, features)


def solution(mesh):
    in_specs = (
        P("parts"),
        P(("parts", "replica")),
        P("parts"),
        P("parts"),
        P(("parts", "replica"), "tensor"),
        P(("parts", "replica"), None, "tensor"),
        P(("parts", "replica"), None, "tensor"),
        P("tensor", None),
        P("tensor", None),
        P(None, "tensor"),
        P("tensor", "parts", None, None),
    )
    out_specs = P(("parts", "replica"), None, "tensor")
    return jax.shard_map(
        on_device, mesh=mesh, in_specs=in_specs, out_specs=out_specs, check_vma=False
    )
```

profile of v0, /device:TPU:0, one launch (start us, length us, event | category | flops | bytes accessed | tf_op | source)
XLA Modules:
  0.0 141.5 jit_solution(18003874679341725483)
XLA Ops:
  0.0 0.0 copy-start
  0.0 1.4 fusion.3
  1.4 2.0 %fusion.4 = s32[]{:T(128)} fusion(s32[4]{0:T(128)} %param.14, s32[]{:T(128)} %fusion.3), kind=kLoop, calls=%fused_computation.31 | loop fusion | flops 11 | bytes 24 | tf_op jit(solution)/shard_map/reduce_sum | solution.py:436
  3.4 0.7 iota_add_fusion.1
  4.1 0.8 select_reduce_fusion.3
  4.9 0.8 select_reduce_fusion.1
  5.7 0.7 select_reduce_fusion.2
  6.4 0.7 broadcast_bitcast_fusion
  7.1 0.1 select_bitcast_fusion
  7.2 0.7 fusion.2
  8.0 0.1 iota_add_fusion
  8.1 0.1 add.74
  8.2 0.7 broadcast_in_dim.102
  8.9 1.2 select_convert_fusion.far
  10.0 1.2 fusion.1
  11.2 1.1 pad_maximum_fusion.1
  12.3 0.0 copy-done
  12.3 0.0 copy-start.1
  12.4 1.1 reshape.121.query
  13.4 2.5 %reshape.120 = bf16[512,2048]{1,0:T(8,128)(2,1)S(1)} reshape(bf16[128,4,2048]{2,1,0:T(4,128)(2,1)} %param.16) | data formatting | bytes 4194304 | tf_op jit(solution)/shard_map/reshape | solution.py:452
  16.0 0.0 copy-done.1
  16.0 1.7 %pad_maximum_fusion.tok = bf16[640,2048]{1,0:T(8,128)(2,1)} fusion(bf16[512,2048]{1,0:T(8,128)(2,1)S(1)} %reshape.120, bf16[128,2048]{1,0:T(8,128)(2,1)S(1)} %copy-done.1), kind=kLoop, calls=%fused_computation | loop fusion | flops 5242880 | bytes 5242880 | tf_op jit(solution)/shard_map/concatenate | solution.py:452
  17.7 119.8 %fused.1 = bf16[512,2048]{1,0:T(8,128)(2,1)} custom-call(bf16[640,2048]{1,0:T(8,128)(2,1)} %pad_maximum_fusion.tok, bf16[2048,512]{1,0:T(8,128)(2,1)} %wk.1, bf16[2048,512]{1,0:T(8,128)(2,1)} %wv.1, f32[640,128]{1,0:T(8,128)} %get-tuple-element.10.cosine, f32[640,128]{1,0:T(8,128)} %get-tuple-element.11.sine, bf16[512,1024]{1,0:T(8,128)(2,1)} %reshape.121.query, ...), custom_call_target="tpu_custom_call" | custom-call | tf_op jit(solution)/shard_map/fused/pallas_call | solution.py:483
  137.4 4.1 %reshape.124 = bf16[128,4,2048]{2,1,0:T(4,128)(2,1)} reshape(bf16[512,2048]{1,0:T(8,128)(2,1)} %fused.1) | data formatting | bytes 4194304 | tf_op jit(solution)/shard_map/reshape | solution.py:513
  (7 shorter events, 0.1 us)
Async XLA Ops:
  0.0 12.3 %copy-start = (bf16[128,4,1024]{2,1,0:T(4,128)(2,1)S(1)}, bf16[128,4,1024]{2,1,0:T(4,128)(2,1)}, u32[]{:S(2)}) copy-start(bf16[128,4,1024]{2,1,0:T(4,128)(2,1)} %param.17) | copy-start | bytes 3145732
  12.3 3.6 %copy-start.1 = (bf16[128,2048]{1,0:T(8,128)(2,1)S(1)}, bf16[128,2048]{1,0:T(8,128)(2,1)}, u32[]{:S(2)}) copy-start(bf16[128,2048]{1,0:T(8,128)(2,1)} %param.15) | copy-start | bytes 1572868
where the time goes:
time: 142 us
  Pallas kernels  120 us (85%)
  other arithmetic  12.5 us (9%)
  local copies, waits for them, and re-layouts  9.24 us (7%)
    pallas_call x1, Pallas kernels, on_device(): pl.pallas_call(functools.partial(fused, n_tensor, n_replica, steps), name...  120 us
    reshape x1, local copies, waits for them, and re-layouts, on_device(): return decoded.reshape(rows, steps, features)  4.1 us

commit v1 on v0

v1 whole, which is shorter than its diff:
```python
import functools
import math

import jax
import jax.numpy as jnp
from jax import lax
from jax.experimental import pallas as pl
from jax.experimental.pallas import tpu as pltpu
from jax.sharding import PartitionSpec as P

HD = 128


rope_base = 1000000.0


def rotary(vectors, places):
    half = vectors.shape[-1] // 2
    freq = rope_base ** (-(2.0 / vectors.shape[-1]) * jnp.arange(half, dtype=jnp.float32))
    angle = places.astype(jnp.float32)[..., None, None] * freq
    cosine = jnp.cos(angle)
    sine = jnp.sin(angle)
    first = vectors[..., :half]
    second = vectors[..., half:]
    return jnp.concatenate([first * cosine - second * sine, second * cosine + first * sine], -1)


def rotate_round(summed, places, kv_heads):
    number = summed.shape[0]
    turned = rotary(summed[:, : kv_heads * HD].reshape(number, kv_heads, HD), places)
    turned = turned.astype(jnp.bfloat16).reshape(number, kv_heads * HD)
    return jnp.concatenate([turned, summed[:, kv_heads * HD :].astype(jnp.bfloat16)], 1)


def own_pair(packed, head_group, kv_heads):
    key_part = lax.dynamic_slice_in_dim(packed, head_group * HD, HD, 1)
    value_part = lax.dynamic_slice_in_dim(packed, (kv_heads + head_group) * HD, HD, 1)
    return jnp.concatenate([key_part, value_part], 1)


def general(
    prompt_owner,
    fork_map,
    page_table,
    prompt_length,
    span_states,
    decode_states,
    decode_queries,
    key_weight,
    value_weight,
    out_weight,
    page_pool,
):
    replica = lax.axis_index("replica")
    device_rank = lax.axis_index("tensor")
    n_replica = lax.axis_size("replica")
    n_tensor = lax.axis_size("tensor")
    span = span_states.shape[0]
    rows, steps, width = decode_states.shape
    heads_dev = decode_queries.shape[2] // HD
    kv_heads = key_weight.shape[1] // HD
    sharing = n_tensor // kv_heads
    prompts = jnp.arange(n_replica, dtype=jnp.int32)
    own_prompt = jnp.sum(jnp.where(prompts == replica, prompt_owner, 0))
    own_length = jnp.sum(jnp.where(prompts == own_prompt, prompt_length, 0))
    row_hits = fork_map[:, None] == prompts[None, :]
    row_length = jnp.sum(jnp.where(row_hits, prompt_length[None, :], 0), 1)
    positions = jnp.concatenate(
        [
            own_length + jnp.arange(span, dtype=jnp.int32),
            (row_length[:, None] + span + jnp.arange(steps, dtype=jnp.int32)[None, :]).reshape(-1),
        ]
    )
    tokens = jnp.concatenate([span_states, decode_states.reshape(rows * steps, width)], 0)
    projected = jnp.dot(
        tokens, jnp.concatenate([key_weight, value_weight], 1), preferred_element_type=jnp.float32
    )
    share = lax.psum_scatter(projected, "tensor", scatter_dimension=0, tiled=True)
    number = share.shape[0]
    start = device_rank * number
    places = lax.dynamic_slice_in_dim(positions, start, number)
    turned = rotate_round(share, places, kv_heads)
    groups = jnp.stack(
        [own_pair(turned, group_index, kv_heads) for group_index in range(kv_heads)], 0
    )
    outgoing = jnp.repeat(groups, sharing, axis=0)
    paired = lax.all_to_all(outgoing, "tensor", split_axis=0, concat_axis=1, tiled=True).reshape(
        -1, 2 * HD
    )
    arrived = lax.all_gather(paired[:span], "replica", axis=0, tiled=True)
    tail_pair = paired[span:].reshape(rows, steps, 2 * HD)
    pool_pages = page_table.shape[0]
    cpages = pool_pages // n_replica
    page_size = page_pool.shape[2]
    entries = jnp.arange(pool_pages, dtype=jnp.int32)
    page_hits = page_table[None, :] == entries[:, None]
    page_prompt = jnp.sum(jnp.where(page_hits, entries[None, :] // cpages, 0), 1)
    page_slot = jnp.sum(jnp.where(page_hits, entries[None, :] % cpages, 0), 1)
    page_length = jnp.sum(
        jnp.where(page_prompt[:, None] == prompts[None, :], prompt_length[None, :], 0), 1
    )
    visible = (
        page_slot[:, None] * page_size + jnp.arange(page_size, dtype=jnp.int32)[None, :]
        < page_length[:, None]
    )
    pool_prompt = jnp.where(visible, page_prompt[:, None], -1).reshape(-1)
    key_prompt = jnp.concatenate([pool_prompt, jnp.repeat(prompt_owner, span)])
    key_table = jnp.concatenate([page_pool.reshape(-1, 2 * HD), arrived], 0)
    cached_keys = key_table[:, :HD]
    cached_values = key_table[:, HD:]
    scale = 1.0 / math.sqrt(HD)
    causal = jnp.arange(steps)[None, :] <= jnp.arange(steps)[:, None]
    per_block = max(1, min(rows, 512 // (steps * heads_dev)))
    blocks = rows // per_block
    queries = decode_queries.reshape(blocks, per_block, steps, heads_dev, HD)

    def attend(items):
        query, prompt, own_tail = items
        flat = query.reshape(-1, HD)
        scores = (
            lax.dot_general(
                flat, cached_keys, (((1,), (1,)), ((), ())), preferred_element_type=jnp.float32
            )
            * scale
        )
        scores = scores.reshape(per_block, steps, heads_dev, -1)
        allowed = (key_prompt[None, :] == prompt[:, None])[:, None, None, :]
        scores = jnp.where(allowed, scores, -jnp.inf)
        tail_scores = (
            jnp.einsum(
                "rshd,rtd->rsht", query, own_tail[..., :HD], preferred_element_type=jnp.float32
            )
            * scale
        )
        tail_scores = jnp.where(causal[None, :, None, :], tail_scores, -jnp.inf)
        highest = jnp.maximum(jnp.max(scores, -1), jnp.max(tail_scores, -1))
        weight = jnp.exp(scores - highest[..., None])
        tail_weight = jnp.exp(tail_scores - highest[..., None])
        total = jnp.sum(weight, -1) + jnp.sum(tail_weight, -1)
        rounded = weight.astype(jnp.bfloat16).reshape(-1, weight.shape[-1])
        mixed = jnp.dot(rounded, cached_values, preferred_element_type=jnp.float32).reshape(
            per_block, steps, heads_dev, HD
        )
        mixed = mixed + jnp.einsum(
            "rsht,rtd->rshd",
            tail_weight.astype(jnp.bfloat16),
            own_tail[..., HD:],
            preferred_element_type=jnp.float32,
        )
        return (mixed / total[..., None]).astype(jnp.bfloat16)

    attended = lax.map(
        attend,
        (
            queries,
            fork_map.reshape(blocks, per_block),
            tail_pair.reshape(blocks, per_block, steps, 2 * HD),
        ),
    )
    head_rows = attended.reshape(rows * steps, heads_dev * HD)
    decoded = jnp.dot(
        lax.all_gather(head_rows, "tensor", axis=1, tiled=True),
        out_weight,
        preferred_element_type=jnp.float32,
    )
    return decoded.astype(jnp.bfloat16).reshape(rows, steps, width)


MESH_ID = pl.DeviceIdType.MESH
TILE = 128
FAR = -(2.0**100)


def nt(left, right):
    return lax.dot_general(
        left, right, (((1,), (1,)), ((), ())), preferred_element_type=jnp.float32
    )


def fused(
    n, n_rep, steps, owner_s, length_s, table_s, fork, span_hbm, dec_hbm, query_hbm, wk_hbm,
    wv_hbm, w_hbm, pool_hbm, out,
    span_tok, dec_tok, query_in, query, w_kv, w_all, pool, hot, cosine, sine,
    part, own, landed, proj, hop_out, hop_in, keys, values, new_keys, new_values,
    mixed, top, gathered, acc,
    in_sem, sp_send, sp_recv, rs_send, rs_recv, nk_send, nk_recv, ag_send, ag_recv, re_send,
):
    z = lax.axis_index("tensor")
    rep = lax.axis_index("replica")
    bf16, f32 = jnp.bfloat16, jnp.float32
    span, depth = span_tok.shape
    rows = dec_tok.shape[0]
    number = rows * steps
    chunks = number // TILE
    group = TILE // steps
    width = query.shape[1]
    heads = width // HD
    pairs = heads // 2
    pages, page_size = pool.shape[0], pool.shape[1]
    cpages = pages // n_rep
    features = w_all.shape[1]
    two = 2 * HD
    factor = math.log2(math.e) / math.sqrt(HD)

    def at(block):
        if isinstance(block, int):
            return pl.ds(block * TILE, TILE)
        return pl.ds(pl.multiple_of(block * TILE, TILE), TILE)

    def load(src, dst, slot):
        return pltpu.make_async_copy(src, dst, in_sem.at[slot])

    loads = [load(span_hbm, span_tok, 0)]
    for d in range(n):
        column = pl.ds(d * HD, HD)
        loads.append(load(wk_hbm.at[:, column], w_kv.at[:, pl.ds(d * two, HD)], 1 + 2 * d))
        loads.append(load(wv_hbm.at[:, column], w_kv.at[:, pl.ds(d * two + HD, HD)], 2 + 2 * d))
    first_dec = len(loads)
    for c in range(chunks):
        piece = pl.ds(c * group, group)
        loads.append(load(dec_hbm.at[piece], dec_tok.at[piece], first_dec + c))
    pool_load = load(pool_hbm, pool, first_dec + chunks)
    query_load = load(query_hbm, query_in, first_dec + chunks + 1)
    w_load = load(w_hbm, w_all, first_dec + chunks + 2)
    for item in loads:
        item.start()
    pool_load.start()
    query_load.start()

    barrier = pltpu.get_barrier_semaphore()
    for k in range(1, n):
        pl.semaphore_signal(
            barrier, inc=1, device_id={"tensor": lax.rem(z + k, n)}, device_id_type=MESH_ID
        )
    for k in range(1, n_rep):
        pl.semaphore_signal(
            barrier, inc=1, device_id={"replica": lax.rem(rep + k, n_rep)}, device_id_type=MESH_ID
        )

    def turns(places, block):
        lane = lax.broadcasted_iota(jnp.int32, (TILE, HD), 1)
        half = HD // 2
        low = lane < half
        power = jnp.where(low, lane, lane - half).astype(f32) * (-(2.0 / HD) * math.log(rope_base))
        angle = places * jnp.exp(power)
        cosine[at(block), :] = jnp.cos(angle)
        turned = jnp.sin(angle)
        sine[at(block), :] = jnp.where(low, -turned, turned)

    own_length = length_s[owner_s[rep]]
    for block in range(span // TILE):
        line = lax.broadcasted_iota(jnp.int32, (TILE, HD), 0)
        turns((line + (own_length + block * TILE)).astype(f32), block)

    for item in loads[:first_dec]:
        item.wait()
    pl.semaphore_wait(barrier, n + n_rep - 2)
    for block in range(span // TILE):
        term = jnp.dot(span_tok[at(block), :], w_kv[...], preferred_element_type=f32)
        for d in range(n):
            part[d, at(block), :] = term[:, d * two : (d + 1) * two].astype(bf16)
            own[d, at(block), :] = term[:, d * two : (d + 1) * two]

    def ahead(side, distance):
        return z + distance if side == 0 else z - distance

    def behind(side, distance):
        return ahead(1 - side, distance)

    def on_line(place):
        return (place >= 0) & (place < n)

    def sp_copy(side, distance):
        target = ahead(side, distance)
        return pltpu.make_async_remote_copy(
            src_ref=part.at[target],
            dst_ref=landed.at[side, distance - 1],
            send_sem=sp_send.at[side, distance - 1],
            recv_sem=sp_recv.at[side, distance - 1],
            device_id={"tensor": target},
            device_id_type=MESH_ID,
        )

    def sp_arrival(side, distance):
        return pltpu.make_async_remote_copy(
            src_ref=part.at[0],
            dst_ref=landed.at[side, distance - 1],
            send_sem=sp_send.at[side, distance - 1],
            recv_sem=sp_recv.at[side, distance - 1],
            device_id={"tensor": lax.rem(z + 1, n)},
            device_id_type=MESH_ID,
        )

    for distance in range(n - 1, 0, -1):
        for side in (0, 1):

            @pl.when(on_line(ahead(side, distance)))
            def _():
                sp_copy(side, distance).start()

    w_load.start()

    def hop(side, c, d):
        return pltpu.make_async_remote_copy(
            src_ref=hop_out.at[side, c, d],
            dst_ref=hop_in.at[side, c, d],
            send_sem=rs_send.at[side, c, d],
            recv_sem=rs_recv.at[side, c, d],
            device_id={"tensor": jnp.clip(ahead(side, 1), 0, n - 1)},
            device_id_type=MESH_ID,
        )

    def onward(side):
        return range(n - 1, 0, -1) if side == 0 else range(0, n - 1)

    def beyond(side, d):
        return d > z if side == 0 else d < z

    def is_end(side):
        return z == 0 if side == 0 else z == n - 1

    def project(c):
        loads[first_dec + c].wait()
        tokens = dec_tok[pl.ds(c * group, group)].reshape(TILE, depth)
        term = jnp.dot(tokens, w_kv[...], preferred_element_type=f32)
        for d in range(n):
            proj[c, d] = term[:, d * two : (d + 1) * two]

        for side in (0, 1):

            @pl.when(is_end(side))
            def _():
                for d in onward(side):
                    hop_out[side, c, d] = proj[c, d].astype(bf16)
                    hop(side, c, d).start()

    def relay(c, side, node):
        @pl.when(z == node)
        def _():
            for d in onward(side):
                if (d > node) if side == 0 else (d < node):
                    hop(side, c, d).wait_recv()
                    total = proj[c, d] + hop_in[side, c, d].astype(f32)
                    hop_out[side, c, d] = total.astype(bf16)
                    hop(side, c, d).start()

    def relay_step(c, k):
        relay(c, 0, k)
        relay(c, 1, n - 1 - k)

    def rotate(total, block):
        key = total[:, :HD]
        key = key * cosine[at(block), :] + pltpu.roll(key, HD // 2, 1) * sine[at(block), :]
        return key.astype(bf16), total[:, HD:].astype(bf16)

    for c in range(chunks):
        project(c)

    prompt_of = lax.broadcasted_iota(jnp.int32, (HD, rows), 0)
    chosen = (prompt_of == fork[...]).astype(f32).astype(bf16)
    lanes = lax.broadcasted_iota(jnp.int32, (TILE, HD), 1)
    lines = lax.broadcasted_iota(jnp.int32, (TILE, HD), 0)
    lengths = jnp.zeros((TILE, HD), f32)
    for p in range(n_rep):
        lengths = jnp.where(lanes == p, length_s[p].astype(f32), lengths)
    for c in range(chunks):
        line = lax.broadcasted_iota(jnp.int32, (TILE, rows), 0)
        lane = lax.broadcasted_iota(jnp.int32, (TILE, rows), 1)
        belongs = (line // steps + c * group == lane).astype(f32).astype(bf16)
        one_hot = nt(belongs, chosen)
        hot[at(c), :] = one_hot.astype(bf16)
        length = jnp.sum(one_hot * lengths, 1, keepdims=True)
        turns(length + (lines % steps + span).astype(f32), c + span // TILE)

    pool_load.wait()
    for j in range(pages):
        p = j // cpages
        start = (j % cpages) * page_size
        place = pl.ds(j * page_size, page_size)
        page = pool[table_s[j]]
        line = lax.broadcasted_iota(jnp.int32, (page_size, HD), 0)
        lane = lax.broadcasted_iota(jnp.int32, (page_size, HD), 1)
        seen = (lane == p) & (line + start < length_s[p])
        keys[place, :HD] = page[:, :HD]
        keys[place, HD:] = jnp.where((lane >= n_rep) | seen, 0.0, FAR).astype(bf16)
        values[place, :HD] = page[:, HD:]
        values[place, HD:] = jnp.ones((page_size, HD), bf16)

    fresh = n_rep * span
    for r in range(n_rep):
        lane = lax.broadcasted_iota(jnp.int32, (span, HD), 1)
        place = pl.ds(r * span, span)
        near = (lane >= n_rep) | (lane == owner_s[r])
        new_keys[place, HD:] = jnp.where(near, 0.0, FAR).astype(bf16)
    new_keys[pl.ds(fresh, TILE), HD:] = jnp.zeros((TILE, HD), bf16)
    new_values[:, HD:] = jnp.ones((new_values.shape[0], HD), bf16)

    query_load.wait()
    for c in range(chunks):
        query[at(c), :] = query_in[pl.ds(c * group, group)].reshape(TILE, width)

    def asked(c, pair):
        asks = []
        for k in range(2):
            column = pl.ds(pl.multiple_of((2 * pair + k) * HD, HD), HD)
            asks.append(jnp.concatenate([query[at(c), column], hot[at(c), :]], 1))
        return jnp.concatenate(asks, 0)

    def cached_part(c):
        @pl.loop(0, pairs)
        def _(pair):
            scores = nt(asked(c, pair), keys[...])
            highest = jnp.max(scores, 1, keepdims=True)
            weight = jnp.exp2((scores - highest) * factor).astype(bf16)
            mixed[c * pairs + pair] = jnp.dot(weight, values[...], preferred_element_type=f32)
            top[c * pairs + pair] = jnp.broadcast_to(highest, (2 * TILE, HD))

    def nk_copy(array, kind, k, whose):
        place = pl.ds(pl.multiple_of(whose * span, span), span)
        return pltpu.make_async_remote_copy(
            src_ref=array.at[place, pl.ds(0, HD)],
            dst_ref=array.at[place, pl.ds(0, HD)],
            send_sem=nk_send.at[kind, k - 1],
            recv_sem=nk_recv.at[kind, k - 1],
            device_id={"replica": lax.rem(rep + k, n_rep)},
            device_id_type=MESH_ID,
        )

    def finish_span():
        for side in (0, 1):
            for distance in range(1, n):

                @pl.when(on_line(behind(side, distance)))
                def _():
                    sp_arrival(side, distance).wait_recv()
                    own[z] = own[z] + landed[side, distance - 1].astype(f32)

        for block in range(span // TILE):
            key, value = rotate(own[z, at(block), :], block)
            place = pl.ds(pl.multiple_of(rep * span + block * TILE, TILE), TILE)
            new_keys[place, :HD] = key
            new_values[place, :HD] = value
        for k in range(1, n_rep):
            nk_copy(new_keys, 0, k, rep).start()
            nk_copy(new_values, 1, k, rep).start()

    def wait_span():
        for k in range(1, n_rep):
            whose = lax.rem(rep - k + n_rep, n_rep)
            nk_copy(new_keys, 0, k, whose).wait_recv()
            nk_copy(new_values, 1, k, whose).wait_recv()

    def finish_tail(c):
        for side in (0, 1):

            @pl.when(jnp.logical_not(is_end(side)))
            def _():
                for d in range(n):

                    @pl.when(z == d)
                    def _():
                        if d != (0 if side == 0 else n - 1):
                            hop(side, c, d).wait_recv()
                            proj[c, d] = proj[c, d] + hop_in[side, c, d].astype(f32)

        key, value = rotate(proj[c, z], c + span // TILE)
        new_keys[pl.ds(fresh, TILE), :HD] = key
        new_values[pl.ds(fresh, TILE), :HD] = value

    half_heads = width // 2

    def block_of(origin, c, half):
        column = pl.ds(half * half_heads, half_heads)
        return gathered.at[origin, at(c), column]

    def ag_copy(side, distance, c, half):
        return pltpu.make_async_remote_copy(
            src_ref=block_of(z, c, half),
            dst_ref=block_of(z, c, half),
            send_sem=ag_send.at[side, distance - 1, c, half],
            recv_sem=ag_recv.at[side, distance - 1, c, half],
            device_id={"tensor": jnp.clip(ahead(side, distance), 0, n - 1)},
            device_id_type=MESH_ID,
        )

    def ag_relay(side, distance, c, half):
        origin = behind(side, distance)
        return pltpu.make_async_remote_copy(
            src_ref=block_of(origin, c, half),
            dst_ref=block_of(origin, c, half),
            send_sem=re_send.at[side, distance - 1, c, half],
            recv_sem=ag_recv.at[side, distance, c, half],
            device_id={"tensor": jnp.clip(ahead(side, 1), 0, n - 1)},
            device_id_type=MESH_ID,
        )

    def ag_arrival(side, distance, c, half):
        origin = behind(side, distance)
        return pltpu.make_async_remote_copy(
            src_ref=block_of(origin, c, half),
            dst_ref=block_of(origin, c, half),
            send_sem=ag_send.at[side, 0, c, half],
            recv_sem=ag_recv.at[side, distance - 1, c, half],
            device_id={"tensor": jnp.clip(ahead(side, 1), 0, n - 1)},
            device_id_type=MESH_ID,
        )

    def sends_to(side, distance):
        place = ahead(side, distance)
        inner = (place <= n - 2) if side == 0 else (place >= 1)
        if distance == 1:
            inner = inner | ((z == n - 2) if side == 0 else (z == 1))
        return inner & on_line(place)

    def relays(side):
        return (z == n - 2) if side == 0 else (z == 1)

    causal_line = lax.broadcasted_iota(jnp.int32, (2 * TILE, TILE), 0)
    causal_lane = lax.broadcasted_iota(jnp.int32, (2 * TILE, TILE), 1)
    causal_line = jnp.where(causal_line >= TILE, causal_line - TILE, causal_line)
    causal = (causal_line // steps == causal_lane // steps) & (causal_lane <= causal_line)

    def new_part(c):
        for half in range(2):

            @pl.loop(half * (pairs // 2), (half + 1) * (pairs // 2))
            def _(pair):
                scores = nt(asked(c, pair), new_keys[...])
                plain = scores[:, :fresh]
                tail = jnp.where(causal, scores[:, fresh:], FAR)
                before = top[c * pairs + pair][:, :1]
                highest = jnp.maximum(
                    jnp.maximum(before, jnp.max(plain, 1, keepdims=True)),
                    jnp.max(tail, 1, keepdims=True),
                )
                weight = jnp.exp2((plain - highest) * factor).astype(bf16)
                tail_weight = jnp.exp2((tail - highest) * factor).astype(bf16)
                weight = jnp.concatenate([weight, tail_weight], 1)
                total = mixed[c * pairs + pair] * jnp.exp2((before - highest) * factor)
                total = total + jnp.dot(weight, new_values[...], preferred_element_type=f32)
                result = (total[:, :HD] / total[:, HD:]).astype(bf16)
                for k in range(2):
                    column = pl.ds(pl.multiple_of((2 * pair + k) * HD, HD), HD)
                    gathered[z, at(c), column] = result[k * TILE : (k + 1) * TILE]

            for distance in range(max(1, n - 2), 0, -1):
                for side in (0, 1):

                    @pl.when(sends_to(side, distance))
                    def _():
                        ag_copy(side, distance, c, half).start()

    cached_part(0)
    for k in range(1, n - 1):
        relay_step(0, k)
    finish_span()
    for c in range(1, chunks):
        cached_part(c)
        for k in range(1, n - 1):
            relay_step(c, k)
    wait_span()
    for c in range(chunks):
        finish_tail(c)
        new_part(c)

    w_load.wait()
    wide = min(512, features)

    def add(origin, block, size, first, last):
        place = pl.ds(pl.multiple_of(block * size, size), size)
        deep = pl.ds(pl.multiple_of(origin * width, width), width)

        @pl.loop(0, features // wide)
        def _(column):
            cols = pl.ds(pl.multiple_of(column * wide, wide), wide)
            term = jnp.dot(
                gathered[origin, place, :], w_all[deep, cols], preferred_element_type=f32
            )
            if first:
                acc[place, cols] = term
            else:
                acc[place, cols] += term

    tall = min(2 * TILE, number)

    @pl.loop(0, number // tall)
    def _(block):
        add(z, block, tall, True, False)

    @pl.loop(0, chunks)
    def _(c):
        for distance in range(1, n):
            for side in (0, 1):

                @pl.when(on_line(behind(side, distance)))
                def _():
                    for half in range(2):
                        ag_arrival(side, distance, c, half).wait_recv()
                        if distance < n - 1:

                            @pl.when(relays(side))
                            def _():
                                ag_relay(side, distance, c, half).start()

                    add(behind(side, distance), c, TILE, False, False)

        place = pl.ds(c * group, group)

        @pl.loop(0, features // wide)
        def _(column):
            cols = pl.ds(pl.multiple_of(column * wide, wide), wide)
            done = acc[at(c), cols].astype(bf16)
            out[place, :, cols] = done.reshape(group, steps, wide)

    for distance in range(1, n):
        for side in (0, 1):

            @pl.when(on_line(ahead(side, distance)))
            def _():
                sp_copy(side, distance).wait_send()

    for k in range(1, n_rep):
        nk_copy(new_keys, 0, k, rep).wait_send()
        nk_copy(new_values, 1, k, rep).wait_send()
    for side in (0, 1):
        for d in onward(side):

            @pl.when(beyond(side, d))
            def _():
                @pl.loop(0, chunks)
                def _(c):
                    hop(side, c, d).wait_send()

        for distance in range(1, max(2, n - 1)):

            @pl.when(sends_to(side, distance))
            def _():
                @pl.loop(0, chunks)
                def _(c):
                    for half in range(2):
                        ag_copy(side, distance, c, half).wait_send()

        for distance in range(1, n - 1):

            @pl.when(relays(side) & on_line(behind(side, distance)))
            def _():
                @pl.loop(0, chunks)
                def _(c):
                    for half in range(2):
                        ag_relay(side, distance, c, half).wait_send()


def on_device(
    prompt_owner,
    fork_map,
    page_table,
    prompt_length,
    span_states,
    decode_states,
    decode_queries,
    key_weight,
    value_weight,
    out_weight,
    page_pool,
):
    n_replica = lax.axis_size("replica")
    n_tensor = lax.axis_size("tensor")
    span = span_states.shape[0]
    rows, steps, width = decode_states.shape
    heads_width = decode_queries.shape[2]
    heads_dev = heads_width // HD
    kv_heads = key_weight.shape[1] // HD
    number = rows * steps
    if (
        kv_heads != n_tensor
        or n_tensor < 2
        or n_replica < 2
        or span % TILE
        or number % TILE
        or number % min(2 * TILE, number)
        or TILE % steps
        or heads_dev % 4
        or n_replica > HD
    ):
        return general(
            prompt_owner, fork_map, page_table, prompt_length, span_states, decode_states,
            decode_queries, key_weight, value_weight, out_weight, page_pool,
        )
    features = out_weight.shape[1]
    pages, page_size = page_pool.shape[1], page_pool.shape[2]
    cached = pages * page_size
    fresh = n_replica * span + TILE
    chunks = number // TILE
    two = 2 * HD
    pairs = chunks * heads_dev // 2
    inner = max(1, n_tensor - 2)
    bf16, f32 = jnp.bfloat16, jnp.float32
    dma = pltpu.SemaphoreType.DMA
    vmem, smem = pltpu.VMEM, pl.BlockSpec(memory_space=pltpu.SMEM)
    whole = pl.BlockSpec(memory_space=pltpu.VMEM)
    return pl.pallas_call(
        functools.partial(fused, n_tensor, n_replica, steps),
        name="fused",
        out_shape=jax.ShapeDtypeStruct((rows, steps, features), bf16),
        in_specs=[smem] * 3 + [whole] + [pl.BlockSpec(memory_space=pl.ANY)] * 7,
        out_specs=whole,
        scratch_shapes=[
            vmem(span_states.shape, bf16),
            vmem(decode_states.shape, bf16),
            vmem(decode_queries.shape, bf16),
            vmem((number, heads_width), bf16),
            vmem((width, n_tensor * two), bf16),
            vmem(out_weight.shape, bf16),
            vmem(page_pool.shape[1:], bf16),
            vmem((number, HD), bf16),
            vmem((span + number, HD), f32),
            vmem((span + number, HD), f32),
            vmem((n_tensor, span, two), bf16),
            vmem((n_tensor, span, two), f32),
            vmem((2, n_tensor - 1, span, two), bf16),
            vmem((chunks, n_tensor, TILE, two), f32),
            vmem((2, chunks, n_tensor, TILE, two), bf16),
            vmem((2, chunks, n_tensor, TILE, two), bf16),
            vmem((cached, two), bf16),
            vmem((cached, two), bf16),
            vmem((fresh, two), bf16),
            vmem((fresh, two), bf16),
            vmem((pairs, 2 * TILE, two), f32),
            vmem((pairs, 2 * TILE, HD), f32),
            vmem((n_tensor, number, heads_width), bf16),
            vmem((number, features), f32),
            dma((2 * n_tensor + chunks + 4,)),
            dma((2, n_tensor - 1)),
            dma((2, n_tensor - 1)),
            dma((2, chunks, n_tensor)),
            dma((2, chunks, n_tensor)),
            dma((2, n_replica - 1)),
            dma((2, n_replica - 1)),
            dma((2, inner, chunks, 2)),
            dma((2, n_tensor - 1, chunks, 2)),
            dma((2, inner, chunks, 2)),
        ],
        compiler_params=pltpu.CompilerParams(
            collective_id=0, has_side_effects=True, vmem_limit_bytes=62 * 1024 * 1024
        ),
    )(
        prompt_owner, prompt_length, page_table, fork_map.reshape(1, rows), span_states,
        decode_states, decode_queries, key_weight, value_weight, out_weight,
        page_pool.reshape(page_pool.shape[1:]),
    )


def solution(mesh):
    in_specs = (
        P("parts"),
        P(("parts", "replica")),
        P("parts"),
        P("parts"),
        P(("parts", "replica"), "tensor"),
        P(("parts", "replica"), None, "tensor"),
        P(("parts", "replica"), None, "tensor"),
        P("tensor", None),
        P("tensor", None),
        P(None, "tensor"),
        P("tensor", "parts", None, None),
    )
    out_specs = P(("parts", "replica"), None, "tensor")
    return jax.shard_map(
        on_device, mesh=mesh, in_specs=in_specs, out_specs=out_specs, check_vma=False
    )
```

time: 142 us -> 121 us (0.85)
  other arithmetic: 12.5 us -> 0 us
  local copies, waits for them, and re-layouts: 9.24 us -> 3.92 us
  Pallas kernels: 120 us -> 117 us
    reshape x4 -> x0, local copies, waits for them, and re-layouts: 8.44 us -> none  [the longest x1 4.1 us: on_device(): return decoded.reshape(rows, steps, features)]
    reduce_sum x5 -> x0, other arithmetic: 5.67 us -> none  [the longest x1 2.02 us: on_device(): own_length = jnp.sum(jnp.where(prompts == own_prompt, prompt_length, 0))]
    unnamed x4 -> x1, local copies, waits for them, and re-layouts: 0.01 us -> 3.92 us
    concatenate x3 -> x0, other arithmetic: 2.79 us -> none  [the longest x1 1.68 us: on_device(): jnp.concatenate([span_states, decode_states.reshape(number, width)], 0)]
    pallas_call x1, Pallas kernels: 120 us -> 117 us  [on_device(): pl.pallas_call(functools.partial(fused, n_tensor, n_replica, steps), name...]
    convert_element_type x3 -> x0, other arithmetic: 1.91 us -> none  [the longest x1 1.16 us: on_device(): far = jnp.where((lanes[None, :] < n_replica) & (key_prompt[:, None] != la...]
where the time goes in v1:
time: 121 us
  Pallas kernels  117 us (97%)
  local copies, waits for them, and re-layouts  3.92 us (3%)
    pallas_call x1, Pallas kernels, on_device(): pl.pallas_call(functools.partial(fused, n_tensor, n_replica, steps), name...  117 us
    unnamed x1, local copies, waits for them, and re-layouts  3.92 us

profile of v1, /device:TPU:0, one launch (start us, length us, event | category | flops | bytes accessed | tf_op | source)
XLA Modules:
  0.0 121.2 jit_solution(4335775574063749841)
XLA Ops:
  0.0 117.3 %fused.1 = bf16[128,4,2048]{2,1,0:T(4,128)(2,1)} custom-call(s32[4]{0:T(128)} %owner_s.1, s32[4]{0:T(128)} %length_s.1, s32[12]{0:T(128)} %table_s.1, s32[1,128]{1,0:T(1,128)} %bitcast.3, bf16[128,2048]{1,0:T(8,128)(2,1)} %span_hbm.1, bf16[128,4,2048]{2,1,0:T(4,128)(2,1)} %dec_hbm.1, bf16[128,4,1024]{2,1,0:T(4,128)(2,1)} %query_hbm.1, ...), custom_call_target="tpu_custom_call" | custom-call | tf_op jit(solution)/shard_map/fused/pallas_call | solution.py:701
  117.3 3.9 %copy.13 = bf16[128,4,2048]{2,1,0:T(4,128)(2,1)} copy(bf16[128,4,2048]{2,1,0:T(4,128)(2,1)} %fused.1) | data formatting | bytes 4194304

commit v2 on v1

--- a/solution.py
+++ b/solution.py
@@ -181,9 +181,9 @@
     n, n_rep, steps, owner_s, length_s, table_s, fork, span_hbm, dec_hbm, query_hbm, wk_hbm,
     wv_hbm, w_hbm, pool_hbm, out,
     span_tok, dec_tok, query_in, query, w_kv, w_all, pool, hot, cosine, sine,
-    part, own, landed, proj, hop_out, hop_in, keys, values, new_keys, new_values,
-    mixed, top, gathered, acc,
-    in_sem, sp_send, sp_recv, rs_send, rs_recv, nk_send, nk_recv, ag_send, ag_recv, re_send,
+    part, own, landed, hop_out, hop_in, keys, values, new_keys, new_values,
+    mixed, top, gathered, acc, result,
+    in_sem, sp_send, sp_recv, rs_send, rs_recv, nk_send, nk_recv, ag_send, ag_recv, re_send, out_sem,
 ):
     z = lax.axis_index("tensor")
     rep = lax.axis_index("replica")
@@ -255,11 +255,14 @@
     for item in loads[:first_dec]:
         item.wait()
     pl.semaphore_wait(barrier, n + n_rep - 2)
+    def keep(kind, block, tokens):
+        term = jnp.dot(tokens, w_kv[...], preferred_element_type=f32)
+        for d in range(n):
+            part[kind, d, at(block), :] = term[:, d * two : (d + 1) * two].astype(bf16)
+            own[kind, d, at(block), :] = term[:, d * two : (d + 1) * two]
+
     for block in range(span // TILE):
-        term = jnp.dot(span_tok[at(block), :], w_kv[...], preferred_element_type=f32)
-        for d in range(n):
-            part[d, at(block), :] = term[:, d * two : (d + 1) * two].astype(bf16)
-            own[d, at(block), :] = term[:, d * two : (d + 1) * two]
+        keep(0, block, span_tok[at(block), :])
 
     def ahead(side, distance):
         return z + distance if side == 0 else z - distance
@@ -270,91 +273,114 @@
     def on_line(place):
         return (place >= 0) & (place < n)
 
-    def sp_copy(side, distance):
+    def sized(kind):
+        return pl.ds(0, span if kind == 0 else TILE)
+
+    def sp_copy(kind, side, distance):
         target = ahead(side, distance)
         return pltpu.make_async_remote_copy(
-            src_ref=part.at[target],
-            dst_ref=landed.at[side, distance - 1],
-            send_sem=sp_send.at[side, distance - 1],
-            recv_sem=sp_recv.at[side, distance - 1],
+            src_ref=part.at[kind, target, sized(kind)],
+            dst_ref=landed.at[kind, side, distance - 1, sized(kind)],
+            send_sem=sp_send.at[kind, side, distance - 1],
+            recv_sem=sp_recv.at[kind, side, distance - 1],
             device_id={"tensor": target},
             device_id_type=MESH_ID,
         )
 
-    def sp_arrival(side, distance):
+    def sp_arrival(kind, side, distance):
         return pltpu.make_async_remote_copy(
-            src_ref=part.at[0],
-            dst_ref=landed.at[side, distance - 1],
-            send_sem=sp_send.at[side, distance - 1],
-            recv_sem=sp_recv.at[side, distance - 1],
+            src_ref=part.at[kind, 0, sized(kind)],
+            dst_ref=landed.at[kind, side, distance - 1, sized(kind)],
+            send_sem=sp_send.at[kind, side, distance - 1],
+            recv_sem=sp_recv.at[kind, side, distance - 1],
             device_id={"tensor": lax.rem(z + 1, n)},
             device_id_type=MESH_ID,
         )
 
-    for distance in range(n - 1, 0, -1):
+    def direct(kind, side, distance):
+        place = ahead(side, distance)
+        if kind < 2:
+            return on_line(place)
+        return (place >= 1) & (place <= n - 2)
+
+    def scatter(kind):
+        for distance in range(n - 1, 0, -1):
+            for side in (0, 1):
+
+                @pl.when(direct(kind, side, distance))
+                def _():
+                    sp_copy(kind, side, distance).start()
+
+    def collect(kind):
         for side in (0, 1):
-
-            @pl.when(on_line(ahead(side, distance)))
-            def _():
-                sp_copy(side, distance).start()
-
+            for distance in range(1, n):
+
+                arrives = on_line(behind(side, distance))
+                if kind >= 2:
+                    arrives = arrives & (z >= 1) & (z <= n - 2)
+
+                @pl.when(arrives)
+                def _():
+                    sp_arrival(kind, side, distance).wait_recv()
+                    own[kind, z, sized(kind)] = own[kind, z, sized(kind)] + landed[
+                        kind, side, distance - 1, sized(kind)
+                    ].astype(f32)
+
+    def decode_tokens(c):
+        loads[first_dec + c].wait()
+        return dec_tok[pl.ds(c * group, group)].reshape(TILE, depth)
+
+    scatter(0)
+    keep(1, 0, decode_tokens(0))
+    scatter(1)
     w_load.start()
 
-    def hop(side, c, d):
+    def hop(side, c):
         return pltpu.make_async_remote_copy(
-            src_ref=hop_out.at[side, c, d],
-            dst_ref=hop_in.at[side, c, d],
-            send_sem=rs_send.at[side, c, d],
-            recv_sem=rs_recv.at[side, c, d],
+            src_ref=hop_out.at[side, c - 1],
+            dst_ref=hop_in.at[side, c - 1],
+            send_sem=rs_send.at[side, c - 1],
+            recv_sem=rs_recv.at[side, c - 1],
             device_id={"tensor": jnp.clip(ahead(side, 1), 0, n - 1)},
             device_id_type=MESH_ID,
         )
 
-    def onward(side):
-        return range(n - 1, 0, -1) if side == 0 else range(0, n - 1)
-
-    def beyond(side, d):
-        return d > z if side == 0 else d < z
+    def last(side):
+        return n - 1 if side == 0 else 0
 
     def is_end(side):
         return z == 0 if side == 0 else z == n - 1
 
+    def hop_on(side, c, total):
+        hop_out[side, c - 1] = total.astype(bf16)
+        hop(side, c).start()
+
     def project(c):
-        loads[first_dec + c].wait()
-        tokens = dec_tok[pl.ds(c * group, group)].reshape(TILE, depth)
-        term = jnp.dot(tokens, w_kv[...], preferred_element_type=f32)
-        for d in range(n):
-            proj[c, d] = term[:, d * two : (d + 1) * two]
-
+        keep(c + 1, 0, decode_tokens(c))
         for side in (0, 1):
 
             @pl.when(is_end(side))
             def _():
-                for d in onward(side):
-                    hop_out[side, c, d] = proj[c, d].astype(bf16)
-                    hop(side, c, d).start()
-
-    def relay(c, side, node):
-        @pl.when(z == node)
-        def _():
-            for d in onward(side):
-                if (d > node) if side == 0 else (d < node):
-                    hop(side, c, d).wait_recv()
-                    total = proj[c, d] + hop_in[side, c, d].astype(f32)
-                    hop_out[side, c, d] = total.astype(bf16)
-                    hop(side, c, d).start()
+                hop_on(side, c, own[c + 1, last(side), sized(c + 1)])
 
     def relay_step(c, k):
-        relay(c, 0, k)
-        relay(c, 1, n - 1 - k)
+        for side, node in ((0, k), (1, n - 1 - k)):
+
+            @pl.when(z == node)
+            def _():
+                hop(side, c).wait_recv()
+                total = own[c + 1, last(side), sized(c + 1)] + hop_in[side, c - 1].astype(f32)
+                hop_on(side, c, total)
 
     def rotate(total, block):
         key = total[:, :HD]
         key = key * cosine[at(block), :] + pltpu.roll(key, HD // 2, 1) * sine[at(block), :]
         return key.astype(bf16), total[:, HD:].astype(bf16)
 
-    for c in range(chunks):
+    for c in range(1, chunks):
         project(c)
+    for c in range(1, chunks):
+        scatter(c + 1)
 
     prompt_of = lax.broadcasted_iota(jnp.int32, (HD, rows), 0)
     chosen = (prompt_of == fork[...]).astype(f32).astype(bf16)
@@ -402,13 +428,12 @@
     def asked(c, pair):
         asks = []
         for k in range(2):
-            column = pl.ds(pl.multiple_of((2 * pair + k) * HD, HD), HD)
+            column = pl.ds((2 * pair + k) * HD, HD)
             asks.append(jnp.concatenate([query[at(c), column], hot[at(c), :]], 1))
         return jnp.concatenate(asks, 0)
 
     def cached_part(c):
-        @pl.loop(0, pairs)
-        def _(pair):
+        for pair in range(pairs):
             scores = nt(asked(c, pair), keys[...])
             highest = jnp.max(scores, 1, keepdims=True)
             weight = jnp.exp2((scores - highest) * factor).astype(bf16)
@@ -427,16 +452,9 @@
         )
 
     def finish_span():
-        for side in (0, 1):
-            for distance in range(1, n):
-
-                @pl.when(on_line(behind(side, distance)))
-                def _():
-                    sp_arrival(side, distance).wait_recv()
-                    own[z] = own[z] + landed[side, distance - 1].astype(f32)
-
+        collect(0)
         for block in range(span // TILE):
-            key, value = rotate(own[z, at(block), :], block)
+            key, value = rotate(own[0, z, at(block), :], block)
             place = pl.ds(pl.multiple_of(rep * span + block * TILE, TILE), TILE)
             new_keys[place, :HD] = key
             new_values[place, :HD] = value
@@ -450,22 +468,24 @@
             nk_copy(new_keys, 0, k, whose).wait_recv()
             nk_copy(new_values, 1, k, whose).wait_recv()
 
-    def finish_tail(c):
-        for side in (0, 1):
-
-            @pl.when(jnp.logical_not(is_end(side)))
-            def _():
-                for d in range(n):
-
-                    @pl.when(z == d)
-                    def _():
-                        if d != (0 if side == 0 else n - 1):
-                            hop(side, c, d).wait_recv()
-                            proj[c, d] = proj[c, d] + hop_in[side, c, d].astype(f32)
-
-        key, value = rotate(proj[c, z], c + span // TILE)
+    def place_tail(total, c):
+        key, value = rotate(total, c + span // TILE)
         new_keys[pl.ds(fresh, TILE), :HD] = key
         new_values[pl.ds(fresh, TILE), :HD] = value
+
+    def finish_tail(c):
+        collect(c + 1)
+        if c > 0:
+            for side in (0, 1):
+
+                @pl.when(z == last(side))
+                def _():
+                    hop(side, c).wait_recv()
+                    own[c + 1, z, sized(c + 1)] = own[c + 1, z, sized(c + 1)] + hop_in[
+                        side, c - 1
+                    ].astype(f32)
+
+        place_tail(own[c + 1, z, sized(c + 1)], c)
 
     half_heads = width // 2
 
@@ -522,9 +542,7 @@
 
     def new_part(c):
         for half in range(2):
-
-            @pl.loop(half * (pairs // 2), (half + 1) * (pairs // 2))
-            def _(pair):
+            for pair in range(half * (pairs // 2), (half + 1) * (pairs // 2)):
                 scores = nt(asked(c, pair), new_keys[...])
                 plain = scores[:, :fresh]
                 tail = jnp.where(causal, scores[:, fresh:], FAR)
@@ -538,10 +556,10 @@
                 weight = jnp.concatenate([weight, tail_weight], 1)
                 total = mixed[c * pairs + pair] * jnp.exp2((before - highest) * factor)
                 total = total + jnp.dot(weight, new_values[...], preferred_element_type=f32)
-                result = (total[:, :HD] / total[:, HD:]).astype(bf16)
+                mean = (total[:, :HD] / total[:, HD:]).astype(bf16)
                 for k in range(2):
-                    column = pl.ds(pl.multiple_of((2 * pair + k) * HD, HD), HD)
-                    gathered[z, at(c), column] = result[k * TILE : (k + 1) * TILE]
+                    column = pl.ds((2 * pair + k) * HD, HD)
+                    gathered[z, at(c), column] = mean[k * TILE : (k + 1) * TILE]
 
             for distance in range(max(1, n - 2), 0, -1):
                 for side in (0, 1):
@@ -550,45 +568,61 @@
                     def _():
                         ag_copy(side, distance, c, half).start()
 
-    cached_part(0)
-    for k in range(1, n - 1):
-        relay_step(0, k)
+    @pl.loop(0, min(2, chunks))
+    def _(c):
+        cached_part(c)
+
     finish_span()
-    for c in range(1, chunks):
+
+    @pl.loop(2, max(2, chunks))
+    def _(c):
         cached_part(c)
-        for k in range(1, n - 1):
-            relay_step(c, k)
+
+    if n > 2:
+        for c in range(1, chunks):
+            relay_step(c, 1)
     wait_span()
     for c in range(chunks):
         finish_tail(c)
         new_part(c)
+        if c == 0:
+            for k in range(2, n - 1):
+                for other in range(1, chunks):
+                    relay_step(other, k)
 
     w_load.wait()
     wide = min(512, features)
 
-    def add(origin, block, size, first, last):
+    def add(origin, block, size, first, half):
         place = pl.ds(pl.multiple_of(block * size, size), size)
-        deep = pl.ds(pl.multiple_of(origin * width, width), width)
+        extent = width if half is None else half_heads
+        begin = 0 if half is None else half * half_heads
+        deep = pl.ds(pl.multiple_of(origin * width + begin, extent), extent)
 
         @pl.loop(0, features // wide)
         def _(column):
             cols = pl.ds(pl.multiple_of(column * wide, wide), wide)
             term = jnp.dot(
-                gathered[origin, place, :], w_all[deep, cols], preferred_element_type=f32
+                gathered[origin, place, begin : begin + extent],
+                w_all[deep, cols],
+                preferred_element_type=f32,
             )
             if first:
                 acc[place, cols] = term
             else:
                 acc[place, cols] += term
 
+    def out_copy(c):
+        place = pl.ds(c * group, group)
+        return pltpu.make_async_copy(result.at[place], out.at[place], out_sem.at[c])
+
     tall = min(2 * TILE, number)
 
     @pl.loop(0, number // tall)
     def _(block):
-        add(z, block, tall, True, False)
-
-    @pl.loop(0, chunks)
-    def _(c):
+        add(z, block, tall, True, None)
+
+    def output(c):
         for distance in range(1, n):
             for side in (0, 1):
 
@@ -602,7 +636,7 @@
                             def _():
                                 ag_relay(side, distance, c, half).start()
 
-                    add(behind(side, distance), c, TILE, False, False)
+                        add(behind(side, distance), c, TILE, False, half)
 
         place = pl.ds(c * group, group)
 
@@ -610,26 +644,31 @@
         def _(column):
             cols = pl.ds(pl.multiple_of(column * wide, wide), wide)
             done = acc[at(c), cols].astype(bf16)
-            out[place, :, cols] = done.reshape(group, steps, wide)
-
-    for distance in range(1, n):
-        for side in (0, 1):
-
-            @pl.when(on_line(ahead(side, distance)))
-            def _():
-                sp_copy(side, distance).wait_send()
+            result[place, :, cols] = done.reshape(group, steps, wide)
+
+        out_copy(c).start()
+
+    @pl.loop(0, chunks - 1)
+    def _(c):
+        output(c)
+
+    for kind in range(chunks + 1):
+        for distance in range(1, n):
+            for side in (0, 1):
+
+                @pl.when(direct(kind, side, distance))
+                def _():
+                    sp_copy(kind, side, distance).wait_send()
 
     for k in range(1, n_rep):
         nk_copy(new_keys, 0, k, rep).wait_send()
         nk_copy(new_values, 1, k, rep).wait_send()
     for side in (0, 1):
-        for d in onward(side):
-
-            @pl.when(beyond(side, d))
-            def _():
-                @pl.loop(0, chunks)
-                def _(c):
-                    hop(side, c, d).wait_send()
+
+        @pl.when(jnp.logical_not(z == last(side)))
+        def _():
+            for c in range(1, chunks):
+                hop(side, c).wait_send()
 
         for distance in range(1, max(2, n - 1)):
 
@@ -640,6 +679,8 @@
                     for half in range(2):
                         ag_copy(side, distance, c, half).wait_send()
 
+    output(chunks - 1)
+    for side in (0, 1):
         for distance in range(1, n - 1):
 
             @pl.when(relays(side) & on_line(behind(side, distance)))
@@ -648,6 +689,10 @@
                 def _(c):
                     for half in range(2):
                         ag_relay(side, distance, c, half).wait_send()
+
+    @pl.loop(0, chunks)
+    def _(c):
+        out_copy(c).wait()
 
 
 def on_device(
@@ -694,6 +739,7 @@
     two = 2 * HD
     pairs = chunks * heads_dev // 2
     inner = max(1, n_tensor - 2)
+    kinds, later = chunks + 1, max(1, chunks - 1)
     bf16, f32 = jnp.bfloat16, jnp.float32
     dma = pltpu.SemaphoreType.DMA
     vmem, smem = pltpu.VMEM, pl.BlockSpec(memory_space=pltpu.SMEM)
@@ -703,7 +749,7 @@
         name="fused",
         out_shape=jax.ShapeDtypeStruct((rows, steps, features), bf16),
         in_specs=[smem] * 3 + [whole] + [pl.BlockSpec(memory_space=pl.ANY)] * 7,
-        out_specs=whole,
+        out_specs=pl.BlockSpec(memory_space=pl.ANY),
         scratch_shapes=[
             vmem(span_states.shape, bf16),
             vmem(decode_states.shape, bf16),
@@ -715,12 +761,11 @@
             vmem((number, HD), bf16),
             vmem((span + number, HD), f32),
             vmem((span + number, HD), f32),
-            vmem((n_tensor, span, two), bf16),
-            vmem((n_tensor, span, two), f32),
-            vmem((2, n_tensor - 1, span, two), bf16),
-            vmem((chunks, n_tensor, TILE, two), f32),
-            vmem((2, chunks, n_tensor, TILE, two), bf16),
-            vmem((2, chunks, n_tensor, TILE, two), bf16),
+            vmem((kinds, n_tensor, max(span, TILE), two), bf16),
+            vmem((kinds, n_tensor, max(span, TILE), two), f32),
+            vmem((kinds, 2, n_tensor - 1, max(span, TILE), two), bf16),
+            vmem((2, later, TILE, two), bf16),
+            vmem((2, later, TILE, two), bf16),
             vmem((cached, two), bf16),
             vmem((cached, two), bf16),
             vmem((fresh, two), bf16),
@@ -729,16 +774,18 @@
             vmem((pairs, 2 * TILE, HD), f32),
             vmem((n_tensor, number, heads_width), bf16),
             vmem((number, features), f32),
+            vmem((rows, steps, features), bf16),
             dma((2 * n_tensor + chunks + 4,)),
-            dma((2, n_tensor - 1)),
-            dma((2, n_tensor - 1)),
-            dma((2, chunks, n_tensor)),
-            dma((2, chunks, n_tensor)),
+            dma((kinds, 2, n_tensor - 1)),
+            dma((kinds, 2, n_tensor - 1)),
+            dma((2, later)),
+            dma((2, later)),
             dma((2, n_replica - 1)),
             dma((2, n_replica - 1)),
             dma((2, inner, chunks, 2)),
             dma((2, n_tensor - 1, chunks, 2)),
             dma((2, inner, chunks, 2)),
+            dma((chunks,)),
         ],
         compiler_params=pltpu.CompilerParams(
             collective_id=0, has_side_effects=True, vmem_limit_bytes=62 * 1024 * 1024

time: 121 us -> 108 us (0.89)
  Pallas kernels: 117 us -> 104 us
    pallas_call x1, Pallas kernels: 117 us -> 104 us  [on_device(): pl.pallas_call(functools.partial(fused, n_tensor, n_replica, steps), name...]
where the time goes in v2:
time: 108 us
  Pallas kernels  104 us (96%)
  local copies, waits for them, and re-layouts  3.92 us (4%)
    pallas_call x1, Pallas kernels, on_device(): pl.pallas_call(functools.partial(fused, n_tensor, n_replica, steps), name...  104 us
    unnamed x1, local copies, waits for them, and re-layouts  3.92 us

profile of v2, /device:TPU:0, one launch (start us, length us, event | category | flops | bytes accessed | tf_op | source)
XLA Modules:
  0.0 107.8 jit_solution(14979191912374827088)
XLA Ops:
  0.0 103.8 %fused.1 = bf16[128,4,2048]{2,1,0:T(4,128)(2,1)} custom-call(s32[4]{0:T(128)} %owner_s.1, s32[4]{0:T(128)} %length_s.1, s32[12]{0:T(128)} %table_s.1, s32[1,128]{1,0:T(1,128)} %bitcast.3, bf16[128,2048]{1,0:T(8,128)(2,1)} %span_hbm.1, bf16[128,4,2048]{2,1,0:T(4,128)(2,1)} %dec_hbm.1, bf16[128,4,1024]{2,1,0:T(4,128)(2,1)} %query_hbm.1, ...), custom_call_target="tpu_custom_call" | custom-call | tf_op jit(solution)/shard_map/fused/pallas_call | solution.py:747
  103.8 3.9 %copy.13 = bf16[128,4,2048]{2,1,0:T(4,128)(2,1)} copy(bf16[128,4,2048]{2,1,0:T(4,128)(2,1)} %fused.1) | data formatting | bytes 4194304

commit v3 on v2

--- a/solution.py
+++ b/solution.py
@@ -183,7 +183,7 @@
     span_tok, dec_tok, query_in, query, w_kv, w_all, pool, hot, cosine, sine,
     part, own, landed, hop_out, hop_in, keys, values, new_keys, new_values,
     mixed, top, gathered, acc, result,
-    in_sem, sp_send, sp_recv, rs_send, rs_recv, nk_send, nk_recv, ag_send, ag_recv, re_send, out_sem,
+    in_sem, sp_send, sp_recv, rs_send, rs_recv, nk_send, nk_recv, ag_send, ag_recv, out_sem,
 ):
     z = lax.axis_index("tensor")
     rep = lax.axis_index("replica")
@@ -265,7 +265,7 @@
         keep(0, block, span_tok[at(block), :])
 
     def ahead(side, distance):
-        return z + distance if side == 0 else z - distance
+        return z + distance - 2 * side * distance
 
     def behind(side, distance):
         return ahead(1 - side, distance)
@@ -297,17 +297,20 @@
             device_id_type=MESH_ID,
         )
 
+    def inner(place):
+        return (place >= 1) & (place <= n - 2)
+
     def direct(kind, side, distance):
         place = ahead(side, distance)
-        if kind < 2:
-            return on_line(place)
-        return (place >= 1) & (place <= n - 2)
-
-    def scatter(kind):
+        return on_line(place) if kind < 2 else inner(place)
+
+    def scatter(kind, ends):
         for distance in range(n - 1, 0, -1):
             for side in (0, 1):
-
-                @pl.when(direct(kind, side, distance))
+                place = ahead(side, distance)
+                target = on_line(place) & jnp.logical_not(inner(place)) if ends else inner(place)
+
+                @pl.when(target)
                 def _():
                     sp_copy(kind, side, distance).start()
 
@@ -315,11 +318,9 @@
         for side in (0, 1):
             for distance in range(1, n):
 
-                arrives = on_line(behind(side, distance))
-                if kind >= 2:
-                    arrives = arrives & (z >= 1) & (z <= n - 2)
-
-                @pl.when(arrives)
+                here = on_line(behind(side, distance))
+
+                @pl.when(here if kind < 2 else here & inner(z))
                 def _():
                     sp_arrival(kind, side, distance).wait_recv()
                     own[kind, z, sized(kind)] = own[kind, z, sized(kind)] + landed[
@@ -330,17 +331,12 @@
         loads[first_dec + c].wait()
         return dec_tok[pl.ds(c * group, group)].reshape(TILE, depth)
 
-    scatter(0)
-    keep(1, 0, decode_tokens(0))
-    scatter(1)
-    w_load.start()
-
-    def hop(side, c):
+    def hop(side, kind):
         return pltpu.make_async_remote_copy(
-            src_ref=hop_out.at[side, c - 1],
-            dst_ref=hop_in.at[side, c - 1],
-            send_sem=rs_send.at[side, c - 1],
-            recv_sem=rs_recv.at[side, c - 1],
+            src_ref=hop_out.at[side, kind, sized(kind)],
+            dst_ref=hop_in.at[side, kind, sized(kind)],
+            send_sem=rs_send.at[side, kind],
+            recv_sem=rs_recv.at[side, kind],
             device_id={"tensor": jnp.clip(ahead(side, 1), 0, n - 1)},
             device_id_type=MESH_ID,
         )
@@ -348,39 +344,52 @@
     def last(side):
         return n - 1 if side == 0 else 0
 
-    def is_end(side):
-        return z == 0 if side == 0 else z == n - 1
-
-    def hop_on(side, c, total):
-        hop_out[side, c - 1] = total.astype(bf16)
-        hop(side, c).start()
-
-    def project(c):
-        keep(c + 1, 0, decode_tokens(c))
+    def hop_first(kind):
         for side in (0, 1):
 
-            @pl.when(is_end(side))
+            @pl.when(z == last(1 - side))
             def _():
-                hop_on(side, c, own[c + 1, last(side), sized(c + 1)])
-
-    def relay_step(c, k):
+                hop_out[side, kind, sized(kind)] = part[kind, last(side), sized(kind)]
+                hop(side, kind).start()
+
+    def relay_step(kind, k):
         for side, node in ((0, k), (1, n - 1 - k)):
 
             @pl.when(z == node)
             def _():
-                hop(side, c).wait_recv()
-                total = own[c + 1, last(side), sized(c + 1)] + hop_in[side, c - 1].astype(f32)
-                hop_on(side, c, total)
+                hop(side, kind).wait_recv()
+                total = own[kind, last(side), sized(kind)]
+                total = total + hop_in[side, kind, sized(kind)].astype(f32)
+                hop_out[side, kind, sized(kind)] = total.astype(bf16)
+                hop(side, kind).start()
+
+    def arrive_end(kind):
+        for side in (0, 1):
+
+            @pl.when(z == last(side))
+            def _():
+                hop(side, kind).wait_recv()
+                own[kind, z, sized(kind)] = own[kind, z, sized(kind)] + hop_in[
+                    side, kind, sized(kind)
+                ].astype(f32)
+
+    scatter(0, False)
+    keep(1, 0, decode_tokens(0))
+    scatter(1, False)
+    scatter(0, True)
+    scatter(1, True)
+    w_load.start()
+    for c in range(1, chunks):
+        keep(c + 1, 0, decode_tokens(c))
+        scatter(c + 1, False)
+    for c in range(1, chunks):
+        hop_first(c + 1)
 
     def rotate(total, block):
         key = total[:, :HD]
         key = key * cosine[at(block), :] + pltpu.roll(key, HD // 2, 1) * sine[at(block), :]
         return key.astype(bf16), total[:, HD:].astype(bf16)
 
-    for c in range(1, chunks):
-        project(c)
-    for c in range(1, chunks):
-        scatter(c + 1)
 
     prompt_of = lax.broadcasted_iota(jnp.int32, (HD, rows), 0)
     chosen = (prompt_of == fork[...]).astype(f32).astype(bf16)
@@ -476,15 +485,7 @@
     def finish_tail(c):
         collect(c + 1)
         if c > 0:
-            for side in (0, 1):
-
-                @pl.when(z == last(side))
-                def _():
-                    hop(side, c).wait_recv()
-                    own[c + 1, z, sized(c + 1)] = own[c + 1, z, sized(c + 1)] + hop_in[
-                        side, c - 1
-                    ].astype(f32)
-
+            arrive_end(c + 1)
         place_tail(own[c + 1, z, sized(c + 1)], c)
 
     half_heads = width // 2
@@ -494,21 +495,11 @@
         return gathered.at[origin, at(c), column]
 
     def ag_copy(side, distance, c, half):
-        return pltpu.make_async_remote_copy(
-            src_ref=block_of(z, c, half),
-            dst_ref=block_of(z, c, half),
-            send_sem=ag_send.at[side, distance - 1, c, half],
-            recv_sem=ag_recv.at[side, distance - 1, c, half],
-            device_id={"tensor": jnp.clip(ahead(side, distance), 0, n - 1)},
-            device_id_type=MESH_ID,
-        )
-
-    def ag_relay(side, distance, c, half):
         origin = behind(side, distance)
         return pltpu.make_async_remote_copy(
             src_ref=block_of(origin, c, half),
             dst_ref=block_of(origin, c, half),
-            send_sem=re_send.at[side, distance - 1, c, half],
+            send_sem=ag_send.at[side, distance, c, half],
             recv_sem=ag_recv.at[side, distance, c, half],
             device_id={"tensor": jnp.clip(ahead(side, 1), 0, n - 1)},
             device_id_type=MESH_ID,
@@ -525,15 +516,12 @@
             device_id_type=MESH_ID,
         )
 
-    def sends_to(side, distance):
-        place = ahead(side, distance)
-        inner = (place <= n - 2) if side == 0 else (place >= 1)
-        if distance == 1:
-            inner = inner | ((z == n - 2) if side == 0 else (z == 1))
-        return inner & on_line(place)
-
-    def relays(side):
-        return (z == n - 2) if side == 0 else (z == 1)
+    busy = jnp.where(z >= n // 2, 0, 1)
+
+    def send_own(side, c, half):
+        @pl.when(on_line(ahead(side, 1)))
+        def _():
+            ag_copy(side, 0, c, half).start()
 
     causal_line = lax.broadcasted_iota(jnp.int32, (2 * TILE, TILE), 0)
     causal_lane = lax.broadcasted_iota(jnp.int32, (2 * TILE, TILE), 1)
@@ -561,34 +549,40 @@
                     column = pl.ds((2 * pair + k) * HD, HD)
                     gathered[z, at(c), column] = mean[k * TILE : (k + 1) * TILE]
 
-            for distance in range(max(1, n - 2), 0, -1):
-                for side in (0, 1):
-
-                    @pl.when(sends_to(side, distance))
-                    def _():
-                        ag_copy(side, distance, c, half).start()
-
-    @pl.loop(0, min(2, chunks))
-    def _(c):
-        cached_part(c)
-
+            send_own(busy, c, half)
+            if c < 2:
+                send_own(1 - busy, c, half)
+
+    def ask(low, high):
+        @pl.loop(low, max(low, min(high, chunks)))
+        def _(c):
+            cached_part(c)
+
+    ask(0, 1)
     finish_span()
-
-    @pl.loop(2, max(2, chunks))
-    def _(c):
-        cached_part(c)
-
-    if n > 2:
-        for c in range(1, chunks):
-            relay_step(c, 1)
+    ask(1, 3)
     wait_span()
-    for c in range(chunks):
+    finish_tail(0)
+    new_part(0)
+    ask(3, chunks)
+
+    def relay_all(k):
+        for kind in range(2, chunks + 1):
+            relay_step(kind, k)
+
+    for c in range(1, chunks):
         finish_tail(c)
         new_part(c)
-        if c == 0:
-            for k in range(2, n - 1):
-                for other in range(1, chunks):
-                    relay_step(other, k)
+    for k in range(1, n - 1):
+        relay_all(k)
+        if k == 1:
+            for c in range(2, chunks):
+                for half in range(2):
+                    send_own(1 - busy, c, half)
+    if n == 2:
+        for c in range(2, chunks):
+            for half in range(2):
+                send_own(1 - busy, c, half)
 
     w_load.wait()
     wide = min(512, features)
@@ -623,21 +617,6 @@
         add(z, block, tall, True, None)
 
     def output(c):
-        for distance in range(1, n):
-            for side in (0, 1):
-
-                @pl.when(on_line(behind(side, distance)))
-                def _():
-                    for half in range(2):
-                        ag_arrival(side, distance, c, half).wait_recv()
-                        if distance < n - 1:
-
-                            @pl.when(relays(side))
-                            def _():
-                                ag_relay(side, distance, c, half).start()
-
-                        add(behind(side, distance), c, TILE, False, half)
-
         place = pl.ds(c * group, group)
 
         @pl.loop(0, features // wide)
@@ -648,9 +627,25 @@
 
         out_copy(c).start()
 
-    @pl.loop(0, chunks - 1)
-    def _(c):
-        output(c)
+    def arrivals(distance, side, c):
+        @pl.when(on_line(behind(side, distance)))
+        def _():
+            for half in range(2):
+                ag_arrival(side, distance, c, half).wait_recv()
+                if distance < n - 1:
+
+                    @pl.when(on_line(ahead(side, 1)))
+                    def _():
+                        ag_copy(side, distance, c, half).start()
+
+                add(behind(side, distance), c, TILE, False, half)
+
+    for distance in range(1, n - 1):
+        for side in (busy, 1 - busy):
+
+            @pl.loop(0, chunks)
+            def _(c):
+                arrivals(distance, side, c)
 
     for kind in range(chunks + 1):
         for distance in range(1, n):
@@ -667,28 +662,27 @@
 
         @pl.when(jnp.logical_not(z == last(side)))
         def _():
-            for c in range(1, chunks):
-                hop(side, c).wait_send()
-
-        for distance in range(1, max(2, n - 1)):
-
-            @pl.when(sends_to(side, distance))
+            for kind in range(2, chunks + 1):
+                hop(side, kind).wait_send()
+
+            @pl.loop(0, chunks)
+            def _(c):
+                for half in range(2):
+                    ag_copy(side, 0, c, half).wait_send()
+
+        for distance in range(1, n - 1):
+
+            @pl.when(on_line(ahead(side, 1)) & on_line(behind(side, distance)))
             def _():
                 @pl.loop(0, chunks)
                 def _(c):
                     for half in range(2):
                         ag_copy(side, distance, c, half).wait_send()
 
-    output(chunks - 1)
-    for side in (0, 1):
-        for distance in range(1, n - 1):
-
-            @pl.when(relays(side) & on_line(behind(side, distance)))
-            def _():
-                @pl.loop(0, chunks)
-                def _(c):
-                    for half in range(2):
-                        ag_relay(side, distance, c, half).wait_send()
+    @pl.loop(0, chunks)
+    def _(c):
+        arrivals(n - 1, busy, c)
+        output(c)
 
     @pl.loop(0, chunks)
     def _(c):
@@ -738,8 +732,7 @@
     chunks = number // TILE
     two = 2 * HD
     pairs = chunks * heads_dev // 2
-    inner = max(1, n_tensor - 2)
-    kinds, later = chunks + 1, max(1, chunks - 1)
+    kinds = chunks + 1
     bf16, f32 = jnp.bfloat16, jnp.float32
     dma = pltpu.SemaphoreType.DMA
     vmem, smem = pltpu.VMEM, pl.BlockSpec(memory_space=pltpu.SMEM)
@@ -764,8 +757,8 @@
             vmem((kinds, n_tensor, max(span, TILE), two), bf16),
             vmem((kinds, n_tensor, max(span, TILE), two), f32),
             vmem((kinds, 2, n_tensor - 1, max(span, TILE), two), bf16),
-            vmem((2, later, TILE, two), bf16),
-            vmem((2, later, TILE, two), bf16),
+            vmem((2, kinds, max(span, TILE), two), bf16),
+            vmem((2, kinds, max(span, TILE), two), bf16),
             vmem((cached, two), bf16),
             vmem((cached, two), bf16),
             vmem((fresh, two), bf16),
@@ -778,13 +771,12 @@
             dma((2 * n_tensor + chunks + 4,)),
             dma((kinds, 2, n_tensor - 1)),
             dma((kinds, 2, n_tensor - 1)),
-            dma((2, later)),
-            dma((2, later)),
+            dma((2, kinds)),
+            dma((2, kinds)),
             dma((2, n_replica - 1)),
             dma((2, n_replica - 1)),
-            dma((2, inner, chunks, 2)),
             dma((2, n_tensor - 1, chunks, 2)),
-            dma((2, inner, chunks, 2)),
+            dma((2, n_tensor - 1, chunks, 2)),
             dma((chunks,)),
         ],
         compiler_params=pltpu.CompilerParams(

time: 108 us -> 102 us (0.944)
  Pallas kernels: 104 us -> 97.7 us
    pallas_call x1, Pallas kernels: 104 us -> 97.7 us  [on_device(): pl.pallas_call(functools.partial(fused, n_tensor, n_replica, steps), name...]
where the time goes in v3:
time: 102 us
  Pallas kernels  97.7 us (96%)
  local copies, waits for them, and re-layouts  3.92 us (4%)
    pallas_call x1, Pallas kernels, on_device(): pl.pallas_call(functools.partial(fused, n_tensor, n_replica, steps), name...  97.7 us
    unnamed x1, local copies, waits for them, and re-layouts  3.92 us

profile of v3, /device:TPU:0, one launch (start us, length us, event | category | flops | bytes accessed | tf_op | source)
XLA Modules:
  0.0 101.6 jit_solution(17301150558765527848)
XLA Ops:
  0.0 97.7 %fused.1 = bf16[128,4,2048]{2,1,0:T(4,128)(2,1)} custom-call(s32[4]{0:T(128)} %owner_s.1, s32[4]{0:T(128)} %length_s.1, s32[12]{0:T(128)} %table_s.1, s32[1,128]{1,0:T(1,128)} %bitcast.3, bf16[128,2048]{1,0:T(8,128)(2,1)} %span_hbm.1, bf16[128,4,2048]{2,1,0:T(4,128)(2,1)} %dec_hbm.1, bf16[128,4,1024]{2,1,0:T(4,128)(2,1)} %query_hbm.1, ...), custom_call_target="tpu_custom_call" | custom-call | tf_op jit(solution)/shard_map/fused/pallas_call | solution.py:740
  97.7 3.9 %copy.13 = bf16[128,4,2048]{2,1,0:T(4,128)(2,1)} copy(bf16[128,4,2048]{2,1,0:T(4,128)(2,1)} %fused.1) | data formatting | bytes 4194304
